TPU v7x, 32 devices: a whole 2x2x4 slice. The times are simulated.
32 devices in a mesh: grp: 2 (over y), exp: 4 (over z), tp: 4 (over x, core).
Axes of the slice: x: 2, y: 2, z: 4, core: 2. Of those that a mesh axis runs over, the one named last changes fastest.
Arguments:
- tokens: bfloat16 [128, 3584], P(('grp', 'exp'), 'tp'), parts along dimension 0, may hold values from -6 to 6
- gate_up_weight: bfloat16 [3584, 2, 18944], P('tp', None, 'exp'), may hold values from -0.09375 to 0.09375
- down_weight: bfloat16 [18944, 3584], P('exp', 'tp'), may hold values from -0.046875 to 0.046875
- adapter_in: bfloat16 [4, 3584, 16], P('exp', 'tp'), may hold values from -0.09375 to 0.09375
- adapter_out: bfloat16 [4, 16, 3584], P('exp', None, 'tp'), may hold values from -1.5 to 1.5
- expert_ids: int32 [128, 2], P(('grp', 'exp')), parts along dimension 0, may hold values from 0 to 3, all different within a row; in each aligned block of 16 rows (0 to 15, 16 to 31, ...) at most 16 rows name the same one
- route_weight: float32 [128, 2], P(('grp', 'exp')), parts along dimension 0, may hold values from 0.2 to 1
Outputs:
- mixed: bfloat16 [128, 3584], P(('grp', 'exp'), 'tp'), parts along dimension 0
There are 2 independent parts, one for each index of `grp`. A program takes and returns all parts, laid end to end along the dimension named above; an argument that names none is the same for every part. Nothing has to cross between parts.
Inputs may be any that keep to these rules, and one draw needn't show every extreme that they name: `expert_ids`: each row names 2 different experts. Among the 16 rows of one index of exp (aligned blocks of 16 rows) no expert is named by more than 16 rows, and in every draw some expert is named by exactly 16 rows of some block.
All inputs are finite; a program needn't handle non-finite values.
Results may differ from a plain program's by a relative error of at most 0.025.
Values may be sent and summed in bfloat16 or wider, within the bound.
No kernel may reach another device: no remote copies, remote signals or barrier semaphores. Data moves between devices by JAX's collectives and lax.ppermute only.
A program may use at most 64 MiB of HBM per device.

v0:
```python
import jax
import jax.numpy as jnp
from jax import lax
from jax.sharding import PartitionSpec as P


def local(tokens, gate_up_weight, down_weight, adapter_in, adapter_out, expert_ids, route_weight):
    exp_count = lax.axis_size("exp")
    own_rows, feat_width = tokens.shape
    all_tokens = lax.all_gather(tokens, "exp", axis=0, tiled=True)
    hidden_width = gate_up_weight.shape[2]
    pair_weight = gate_up_weight.reshape(feat_width, 2 * hidden_width)
    pair_share = lax.psum_scatter(
        jnp.dot(all_tokens, pair_weight, preferred_element_type=jnp.float32).astype(jnp.bfloat16),
        "tp",
        scatter_dimension=0,
        tiled=True,
    ).astype(jnp.float32)
    hidden_share = (
        jax.nn.silu(pair_share[:, :hidden_width]) * pair_share[:, hidden_width:]
    ).astype(jnp.bfloat16)
    hidden = lax.all_gather(hidden_share, "tp", axis=0, tiled=True)
    base_out = lax.psum_scatter(
        jnp.dot(hidden, down_weight, preferred_element_type=jnp.float32).astype(jnp.bfloat16),
        "exp",
        scatter_dimension=0,
        tiled=True,
    ).astype(jnp.float32)
    top_count = expert_ids.shape[1]
    expert_count = adapter_in.shape[0] * exp_count
    flat_ids = expert_ids.reshape(own_rows * top_count)
    flat_weight = route_weight.reshape(own_rows * top_count)
    expert_hits = (flat_ids[:, None] == jnp.arange(expert_count, dtype=jnp.int32)[None, :]).astype(
        jnp.int32
    )
    capacity = max(2, 2 * top_count * own_rows // expert_count)
    slot_index = jnp.sum((jnp.cumsum(expert_hits, axis=0) - expert_hits) * expert_hits, axis=1)
    slot_target = flat_ids * capacity + slot_index
    slot_hits = (
        slot_target[:, None] == jnp.arange(expert_count * capacity, dtype=jnp.int32)[None, :]
    )
    combine_matrix = jnp.sum(
        (slot_hits.astype(jnp.float32) * flat_weight[:, None]).reshape(
            own_rows, top_count, expert_count * capacity
        ),
        axis=1,
    )
    dispatch_matrix = slot_hits.T.astype(jnp.bfloat16)
    repeated = jnp.repeat(tokens, top_count, axis=0)
    outgoing = jnp.dot(dispatch_matrix, repeated, preferred_element_type=jnp.float32).astype(
        jnp.bfloat16
    )
    outgoing = outgoing.reshape(expert_count, capacity, feat_width)
    rank_partial = jnp.einsum(
        "scd,dr->scr",
        lax.all_to_all(outgoing, "exp", split_axis=0, concat_axis=0, tiled=True),
        adapter_in[0],
        preferred_element_type=jnp.float32,
    )
    rank_mid = lax.psum(rank_partial, "tp").astype(jnp.bfloat16)
    expert_out = jnp.einsum(
        "scr,rd->scd", rank_mid, adapter_out[0], preferred_element_type=jnp.float32
    ).astype(jnp.bfloat16)
    returned = lax.all_to_all(expert_out, "exp", split_axis=0, concat_axis=0, tiled=True)
    adapter_sum = jnp.dot(
        combine_matrix,
        returned.reshape(expert_count * capacity, feat_width).astype(jnp.float32),
        precision=lax.Precision.HIGHEST,
        preferred_element_type=jnp.float32,
    )
    return (base_out + adapter_sum).astype(jnp.bfloat16)


def solution(mesh):
    in_specs = (
        P(("grp", "exp"), "tp"),
        P("tp", None, "exp"),
        P("exp", "tp"),
        P("exp", "tp", None),
        P("exp", None, "tp"),
        P(("grp", "exp"), None),
        P(("grp", "exp"), None),
    )
    out_specs = P(("grp", "exp"), "tp")
    return jax.shard_map(local, mesh=mesh, in_specs=in_specs, out_specs=out_specs, check_vma=False)
```

profile of v0, /device:TPU:0, one launch (start us, length us, event | category | flops | bytes accessed | tf_op | source)
XLA Modules:
  0.0 105.8 jit_solution(269650311221717586)
XLA Ops:
  6.5 0.0 copy-start
  6.5 0.0 reduce-scatter.3.cloned.1.call-start
  6.5 15.4 %all_gather.6 = bf16[64,896]{1,0:T(8,128)(2,1)S(1)} all-gather(bf16[16,896]{1,0:T(8,128)(2,1)} %param.7), channel_id=1, replica_groups=mesh['grp'=2,'exp'=4,'tp'=4] {'exp'}, dimensions={0}, use_global_device_ids=true | all-gather | bytes 143360 | tf_op jit(solution)/shard_map/all_gather | solution.py:10
  22.0 9.7 %copy.22 = bf16[112,8,2,4736]{3,1,2,0:T(8,128)(2,1)S(1)} copy(bf16[112,8,2,4736]{3,2,1,0:T(2,128)(2,1)} %bitcast.22) | data formatting | bytes 33947648
  31.7 0.0 copy-start.3
  31.7 0.0 copy-start.1
  31.7 0.0 copy-start.2
  31.7 3.5 %convolution_convert_fusion = bf16[64,9472]{1,0:T(8,128)(2,1)} fusion(bf16[64,896]{1,0:T(8,128)(2,1)S(1)} %all_gather.6, bf16[896,9472]{1,0:T(8,128)(2,1)S(1)} %bitcast.21), kind=kOutput, calls=%fused_computation | convolution fusion | flops 1086930944 | bytes 18300928 | tf_op jit(solution)/shard_map/dot_general | solution.py:14
  35.2 0.0 reduce-scatter.3.cloned.1.call-update
  35.2 0.0 copy-done.3
  35.2 0.1 copy.20
  35.3 0.1 eq.35
  35.4 0.0 copy-done.1
  35.5 0.1 fusion.6
  35.5 0.1 reduce_window_sum.11
  35.6 0.2 select_reduce_fusion.1
  35.8 1.0 convolution_convert_fusion.2
  36.8 4.8 %all-to-all-start = ((bf16[4,16,896]{2,1,0:T(8,128)(2,1)}), bf16[4,16,896]{2,1,0:T(8,128)(2,1)S(1)}, u32[]{:S(2)}, u32[]{:S(2)}) async-start(bf16[4,16,896]{2,1,0:T(8,128)(2,1)} %bitcast), calls=%async_computation.2 | async-start | bytes 229376 | tf_op jit(solution)/shard_map/all_to_all | solution.py:56
  41.6 0.1 reduce_sum.21
  41.6 0.1 copy.21
  41.7 5.7 %all-to-all-done = bf16[4,16,896]{2,1,0:T(8,128)(2,1)S(1)} async-done(((bf16[4,16,896]{2,1,0:T(8,128)(2,1)}), bf16[4,16,896]{2,1,0:T(8,128)(2,1)S(1)}, u32[]{:S(2)}, u32[]{:S(2)}) %all-to-all-start) | async-done | bytes 114720 | tf_op jit(solution)/shard_map/all_to_all | solution.py:56
  47.4 0.0 copy-done.2
  47.4 0.2 fusion.3
  47.6 11.2 %psum.7 = bf16[4,16,16]{2,1,0:T(8,128)(2,1)S(1)} all-reduce(f32[4,16,16]{2,1,0:T(8,128)S(1)} %fusion.3), channel_id=1, replica_groups=mesh['grp'=2,'exp'=4,'tp'=4] {'tp'}, use_global_device_ids=true, to_apply=%region_5.6 | all-reduce | flops 1024 | bytes 6144 | tf_op jit(solution)/shard_map/psum | solution.py:60
  58.8 0.0 copy-done
  58.8 0.8 convolution_convert_fusion.1
  59.6 3.3 %all-to-all-start.1 = ((bf16[4,16,896]{2,1,0:T(8,128)(2,1)}), bf16[4,16,896]{2,1,0:T(8,128)(2,1)S(1)}, u32[]{:S(2)}, u32[]{:S(2)}) async-start(bf16[4,16,896]{2,1,0:T(8,128)(2,1)} %convolution_convert_fusion.1), calls=%async_computation.3 | async-start | bytes 229376 | tf_op jit(solution)/shard_map/all_to_all | solution.py:64
  62.9 0.0 reduce-scatter.5.cloned.1.call-start
  63.0 0.0 reduce-scatter.3.cloned.1.call-done
  63.0 1.0 convert_element_type.34
  64.0 0.1 fusion.1
  64.1 7.7 %all_gather.7 = bf16[64,4736]{1,0:T(8,128)(2,1)S(1)} all-gather(bf16[16,4736]{1,0:T(8,128)(2,1)S(1)} %fusion.1), channel_id=1, replica_groups=mesh['grp'=2,'exp'=4,'tp'=4] {'tp'}, dimensions={0}, use_global_device_ids=true | all-gather | bytes 757760 | tf_op jit(solution)/shard_map/all_gather | solution.py:22
  71.8 0.0 copy-start.4
  71.8 5.5 %convolution_convert_fusion.3 = bf16[64,896]{1,0:T(8,128)(2,1)} fusion(bf16[64,4736]{1,0:T(8,128)(2,1)S(1)} %all_gather.7, bf16[4736,896]{1,0:T(8,128)(2,1)} %param.9), kind=kOutput, calls=%fused_computation.3 | convolution fusion | flops 543219712 | bytes 9207808 | tf_op jit(solution)/shard_map/dot_general | solution.py:24
  77.3 0.0 reduce-scatter.5.cloned.1.call-update
  77.3 0.0 copy-done.4
  77.3 0.1 select_reduce_fusion
  77.4 0.0 all-to-all-done.1
  77.4 20.0 %reduce-scatter.5.cloned.1.call-done = bf16[16,896]{1,0:T(8,128)(2,1)} async-done(((bf16[64,896]{1,0:T(8,128)(2,1)}), bf16[16,896]{1,0:T(8,128)(2,1)}) %reduce-scatter.5.cloned.1.call-update) | async-done | bytes 28688 | tf_op jit(solution)/shard_map/reduce_scatter | solution.py:23
  97.4 1.5 %fusion = bf16[16,896]{1,0:T(8,128)(2,1)} fusion(f32[16,64]{1,0:T(8,128)S(1)} %select_reduce_fusion, bf16[64,896]{1,0:T(8,128)(2,1)S(1)} %bitcast.23, bf16[16,896]{1,0:T(8,128)(2,1)} %reduce-scatter.5.cloned.1.call-done), kind=kOutput, calls=%fused_computation.5 | convolution fusion | flops 11053056 | bytes 176128 | tf_op jit(solution)/shard_map/dot_general | solution.py:65
  (4 shorter events, 0.1 us)
Async XLA Ops:
  6.5 52.3 %copy-start = (bf16[1,16,896]{2,1,0:T(8,128)(2,1)S(1)}, bf16[1,16,896]{2,1,0:T(8,128)(2,1)}, u32[]{:S(2)}) copy-start(bf16[1,16,896]{2,1,0:T(8,128)(2,1)} %param.11) | copy-start | bytes 86020
  6.5 56.4 %reduce-scatter.3.cloned.1.call-start = ((), (), s32[]{:S(2)}) async-start(), calls=%async_computation.4 | async-start | bytes 1515520 | tf_op jit(solution)/shard_map/reduce_scatter | solution.py:13
  31.7 3.5 %copy-start.3 = (s32[16,2]{0,1:T(2,128)S(1)}, s32[16,2]{0,1:T(2,128)}, u32[]{:S(2)}) copy-start(s32[16,2]{0,1:T(2,128)} %param.12) | copy-start | bytes 388
  31.7 3.7 %copy-start.1 = (bf16[16,896]{1,0:T(8,128)(2,1)S(1)}, bf16[16,896]{1,0:T(8,128)(2,1)}, u32[]{:S(2)}) copy-start(bf16[16,896]{1,0:T(8,128)(2,1)} %param.7) | copy-start | bytes 86020
  31.7 15.7 %copy-start.2 = (bf16[1,896,16]{1,2,0:T(8,128)(2,1)S(1)}, bf16[1,896,16]{1,2,0:T(8,128)(2,1)}, u32[]{:S(2)}) copy-start(bf16[1,896,16]{1,2,0:T(8,128)(2,1)} %param.10) | copy-start | bytes 86020
  36.8 10.7 %all-to-all-start = ((bf16[4,16,896]{2,1,0:T(8,128)(2,1)}), bf16[4,16,896]{2,1,0:T(8,128)(2,1)S(1)}, u32[]{:S(2)}, u32[]{:S(2)}) async-start(bf16[4,16,896]{2,1,0:T(8,128)(2,1)} %bitcast), calls=%async_computation.2 | async-start | bytes 229376 | tf_op jit(solution)/shard_map/all_to_all | solution.py:56
  59.6 17.8 %all-to-all-start.1 = ((bf16[4,16,896]{2,1,0:T(8,128)(2,1)}), bf16[4,16,896]{2,1,0:T(8,128)(2,1)S(1)}, u32[]{:S(2)}, u32[]{:S(2)}) async-start(bf16[4,16,896]{2,1,0:T(8,128)(2,1)} %convolution_convert_fusion.1), calls=%async_computation.3 | async-start | bytes 229376 | tf_op jit(solution)/shard_map/all_to_all | solution.py:64
  62.9 34.5 %reduce-scatter.5.cloned.1.call-start = ((), (), s32[]{:S(2)}) async-start(), calls=%async_computation.5 | async-start | bytes 143360 | tf_op jit(solution)/shard_map/reduce_scatter | solution.py:23
  71.8 5.5 %copy-start.4 = (f32[16,2]{0,1:T(2,128)S(1)}, f32[16,2]{0,1:T(2,128)}, u32[]{:S(2)}) copy-start(f32[16,2]{0,1:T(2,128)} %param.13) | copy-start | bytes 388
Sparse Core Ops, SparseCore 0:
  35.3 27.2 reduce-scatter.2
  77.4 19.9 reduce-scatter.4
where the time goes:
time: 106 us
  blocking collectives  34.4 us (32%)
  waiting for transfers between devices  25.7 us (24%)
  between operations  13.5 us (13%)
  matrix products  12.4 us (12%)
  local copies, waits for them, and re-layouts  10.1 us (10%)
  starting transfers between devices  8.16 us (8%)
  other arithmetic  1.49 us (1%)
    reduce_scatter x1, waiting for transfers between devices, local(): lax.psum_scatter(jnp.dot(hidden, down_weight, preferred_element_type=jnp....  20 us
    all_gather x1, blocking collectives, local(): all_tokens = lax.all_gather(tokens, 'exp', axis=0, tiled=True)  15.4 us
    psum x1, blocking collectives, local(): rank_mid = lax.psum(rank_partial, 'tp').astype(jnp.bfloat16)  11.2 us
    unnamed x12, local copies, waits for them, and re-layouts  9.81 us
    all_gather x1, blocking collectives, local(): hidden = lax.all_gather(hidden_share, 'tp', axis=0, tiled=True)  7.73 us
    all_to_all x1, waiting for transfers between devices, local(): lax.all_to_all(outgoing, 'exp', split_axis=0, concat_axis=0, tiled=True)  5.71 us
    dot_general x1, matrix products, local(): jnp.dot(hidden, down_weight, preferred_element_type=jnp.float32)  5.47 us
    all_to_all x1, starting transfers between devices, local(): lax.all_to_all(outgoing, 'exp', split_axis=0, concat_axis=0, tiled=True)  4.8 us
  transfers between devices with their start and end apart: 4, of which 2 were waited for; matrix products, arithmetic and copies ran while one was open for 9% of the time, Pallas kernels for 0%

commit v1 on v0

--- a/solution.py
+++ b/solution.py
@@ -1,7 +1,17 @@
+import functools
 import jax
 import jax.numpy as jnp
 from jax import lax
 from jax.sharding import PartitionSpec as P
+
+
+def edit_stops_all(row_data, named_axis):
+    aux = jax.lax.all_gather(row_data, named_axis)
+    h_now = jnp.sum(aux, axis=0)
+    return h_now
+
+
+search_row_in = functools.partial(edit_stops_all, named_axis="tp")
 
 
 def local(tokens, gate_up_weight, down_weight, adapter_in, adapter_out, expert_ids, route_weight):
@@ -57,7 +67,7 @@
         adapter_in[0],
         preferred_element_type=jnp.float32,
     )
-    rank_mid = lax.psum(rank_partial, "tp").astype(jnp.bfloat16)
+    rank_mid = search_row_in(rank_partial).astype(jnp.bfloat16)
     expert_out = jnp.einsum(
         "scr,rd->scd", rank_mid, adapter_out[0], preferred_element_type=jnp.float32
     ).astype(jnp.bfloat16)

time: 106 us -> 105 us (level)
  blocking collectives: 34.4 us -> 27.9 us
  waiting for transfers between devices: 25.7 us -> 31 us
    psum x1 -> x0, blocking collectives: 11.2 us -> none  [local(): rank_mid = lax.psum(rank_partial, 'tp').astype(jnp.bfloat16)]
    all_gather x0 -> x1, blocking collectives: none -> 5.42 us  [edit_stops_all(): aux = jax.lax.all_gather(row_data, named_axis)]
    reduce_scatter x1, waiting for transfers between devices: 0.02 us -> 5.19 us  [local(): lax.psum_scatter(jnp.dot(all_tokens, pair_weight, preferred_element_type=...]
  transfers between devices with their start and end apart: 4 -> 4, of which waited for: 2 -> 3; matrix products, arithmetic and copies ran while one was open for 9% -> 9% of each run, Pallas kernels for 0% -> 0%
where the time goes in v1:
time: 105 us
  waiting for transfers between devices  31 us (30%)
  blocking collectives  27.9 us (27%)
  between operations  13.5 us (13%)
  matrix products  12.4 us (12%)
  local copies, waits for them, and re-layouts  10.1 us (10%)
  starting transfers between devices  8.16 us (8%)
  other arithmetic  1.51 us (1%)
    reduce_scatter x1, waiting for transfers between devices, local(): lax.psum_scatter(jnp.dot(hidden, down_weight, preferred_element_type=jnp....  20 us
    all_gather x1, blocking collectives, local(): all_tokens = lax.all_gather(tokens, 'exp', axis=0, tiled=True)  15.4 us
    unnamed x12, local copies, waits for them, and re-layouts  9.81 us
    all_gather x1, blocking collectives, local(): hidden = lax.all_gather(hidden_share, 'tp', axis=0, tiled=True)  7.04 us
    all_to_all x1, waiting for transfers between devices, local(): lax.all_to_all(outgoing, 'exp', split_axis=0, concat_axis=0, tiled=True)  5.71 us
    dot_general x1, matrix products, local(): jnp.dot(hidden, down_weight, preferred_element_type=jnp.float32)  5.46 us
    all_gather x1, blocking collectives, edit_stops_all(): aux = jax.lax.all_gather(row_data, named_axis)  5.42 us
    reduce_scatter x1, waiting for transfers between devices, local(): lax.psum_scatter(jnp.dot(all_tokens, pair_weight, preferred_element_type=...  5.19 us
  transfers between devices with their start and end apart: 4, of which 3 were waited for; matrix products, arithmetic and copies ran while one was open for 9% of the time, Pallas kernels for 0%

profile of v1, /device:TPU:0, one launch (start us, length us, event | category | flops | bytes accessed | tf_op | source)
XLA Modules:
  0.0 104.5 jit_solution(14898736742309367165)
XLA Ops:
  6.5 0.0 copy-start
  6.5 0.0 reduce-scatter.3.cloned.1.call-start
  6.5 15.4 %all_gather.12 = bf16[64,896]{1,0:T(8,128)(2,1)S(1)} all-gather(bf16[16,896]{1,0:T(8,128)(2,1)} %param.7), channel_id=1, replica_groups=mesh['grp'=2,'exp'=4,'tp'=4] {'exp'}, dimensions={0}, use_global_device_ids=true | all-gather | bytes 143360 | tf_op jit(solution)/shard_map/all_gather | solution.py:20
  22.0 9.7 %copy.26 = bf16[112,8,2,4736]{3,1,2,0:T(8,128)(2,1)S(1)} copy(bf16[112,8,2,4736]{3,2,1,0:T(2,128)(2,1)} %bitcast.23) | data formatting | bytes 33947648
  31.7 0.0 copy-start.3
  31.7 0.0 copy-start.1
  31.7 0.0 copy-start.2
  31.7 3.5 %convolution_convert_fusion = bf16[64,9472]{1,0:T(8,128)(2,1)} fusion(bf16[64,896]{1,0:T(8,128)(2,1)S(1)} %all_gather.12, bf16[896,9472]{1,0:T(8,128)(2,1)S(1)} %bitcast.22), kind=kOutput, calls=%fused_computation | convolution fusion | flops 1086930944 | bytes 18300928 | tf_op jit(solution)/shard_map/dot_general | solution.py:24
  35.2 0.0 reduce-scatter.3.cloned.1.call-update
  35.2 0.0 copy-done.3
  35.2 0.1 copy.24
  35.3 0.1 eq.35
  35.4 0.0 copy-done.1
  35.5 0.1 fusion.6
  35.5 0.1 reduce_window_sum.11
  35.6 0.2 select_reduce_fusion.1
  35.8 1.0 convolution_convert_fusion.2
  36.8 4.8 %all-to-all-start = ((bf16[4,16,896]{2,1,0:T(8,128)(2,1)}), bf16[4,16,896]{2,1,0:T(8,128)(2,1)S(1)}, u32[]{:S(2)}, u32[]{:S(2)}) async-start(bf16[4,16,896]{2,1,0:T(8,128)(2,1)} %bitcast), calls=%async_computation.2 | async-start | bytes 229376 | tf_op jit(solution)/shard_map/all_to_all | solution.py:66
  41.6 0.1 reduce_sum.30
  41.6 0.1 copy.25
  41.7 5.7 %all-to-all-done = bf16[4,16,896]{2,1,0:T(8,128)(2,1)S(1)} async-done(((bf16[4,16,896]{2,1,0:T(8,128)(2,1)}), bf16[4,16,896]{2,1,0:T(8,128)(2,1)S(1)}, u32[]{:S(2)}, u32[]{:S(2)}) %all-to-all-start) | async-done | bytes 114720 | tf_op jit(solution)/shard_map/all_to_all | solution.py:66
  47.4 0.0 copy-done.2
  47.4 0.2 fusion.3
  47.6 5.4 %all-gather = f32[16,16,16]{2,1,0:T(8,128)S(1)} all-gather(f32[4,16,16]{2,1,0:T(8,128)S(1)} %fusion.3), channel_id=2, replica_groups=mesh['grp'=2,'exp'=4,'tp'=4] {'tp'}, dimensions={0}, use_global_device_ids=true | all-gather | bytes 20480 | tf_op jit(solution)/shard_map/all_gather | solution.py:9
  53.0 0.0 copy-done
  53.0 0.8 convolution_convert_fusion.1
  53.8 3.3 %all-to-all-start.1 = ((bf16[4,16,896]{2,1,0:T(8,128)(2,1)}), bf16[4,16,896]{2,1,0:T(8,128)(2,1)S(1)}, u32[]{:S(2)}, u32[]{:S(2)}) async-start(bf16[4,16,896]{2,1,0:T(8,128)(2,1)} %convolution_convert_fusion.1), calls=%async_computation.3 | async-start | bytes 229376 | tf_op jit(solution)/shard_map/all_to_all | solution.py:74
  57.2 0.0 reduce-scatter.5.cloned.1.call-start
  57.2 5.2 %reduce-scatter.3.cloned.1.call-done = bf16[16,9472]{1,0:T(8,128)(2,1)} async-done(((bf16[64,9472]{1,0:T(8,128)(2,1)}), bf16[16,9472]{1,0:T(8,128)(2,1)}) %reduce-scatter.3.cloned.1.call-update) | async-done | bytes 303120 | tf_op jit(solution)/shard_map/reduce_scatter | solution.py:23
  62.4 1.0 convert_element_type.34
  63.4 0.1 fusion.1
  63.5 7.0 %all_gather.13 = bf16[64,4736]{1,0:T(8,128)(2,1)S(1)} all-gather(bf16[16,4736]{1,0:T(8,128)(2,1)S(1)} %fusion.1), channel_id=1, replica_groups=mesh['grp'=2,'exp'=4,'tp'=4] {'tp'}, dimensions={0}, use_global_device_ids=true | all-gather | bytes 757760 | tf_op jit(solution)/shard_map/all_gather | solution.py:32
  70.6 0.0 copy-start.4
  70.6 5.5 %convolution_convert_fusion.3 = bf16[64,896]{1,0:T(8,128)(2,1)} fusion(bf16[64,4736]{1,0:T(8,128)(2,1)S(1)} %all_gather.13, bf16[4736,896]{1,0:T(8,128)(2,1)} %param.9), kind=kOutput, calls=%fused_computation.3 | convolution fusion | flops 543219712 | bytes 9207808 | tf_op jit(solution)/shard_map/dot_general | solution.py:34
  76.0 0.0 reduce-scatter.5.cloned.1.call-update
  76.1 0.0 copy-done.4
  76.1 0.1 select_reduce_fusion
  76.1 0.0 all-to-all-done.1
  76.2 20.0 %reduce-scatter.5.cloned.1.call-done = bf16[16,896]{1,0:T(8,128)(2,1)} async-done(((bf16[64,896]{1,0:T(8,128)(2,1)}), bf16[16,896]{1,0:T(8,128)(2,1)}) %reduce-scatter.5.cloned.1.call-update) | async-done | bytes 28688 | tf_op jit(solution)/shard_map/reduce_scatter | solution.py:33
  96.2 1.5 %fusion = bf16[16,896]{1,0:T(8,128)(2,1)} fusion(f32[16,64]{1,0:T(8,128)S(1)} %select_reduce_fusion, bf16[64,896]{1,0:T(8,128)(2,1)S(1)} %bitcast.25, bf16[16,896]{1,0:T(8,128)(2,1)} %reduce-scatter.5.cloned.1.call-done), kind=kOutput, calls=%fused_computation.5 | convolution fusion | flops 11053056 | bytes 176128 | tf_op jit(solution)/shard_map/dot_general | solution.py:75
  (5 shorter events, 0.1 us)
Async XLA Ops:
  6.5 46.5 %copy-start = (bf16[1,16,896]{2,1,0:T(8,128)(2,1)S(1)}, bf16[1,16,896]{2,1,0:T(8,128)(2,1)}, u32[]{:S(2)}) copy-start(bf16[1,16,896]{2,1,0:T(8,128)(2,1)} %param.11) | copy-start | bytes 86020
  6.5 55.9 %reduce-scatter.3.cloned.1.call-start = ((), (), s32[]{:S(2)}) async-start(), calls=%async_computation.4 | async-start | bytes 1515520 | tf_op jit(solution)/shard_map/reduce_scatter | solution.py:23
  31.7 3.5 %copy-start.3 = (s32[16,2]{0,1:T(2,128)S(1)}, s32[16,2]{0,1:T(2,128)}, u32[]{:S(2)}) copy-start(s32[16,2]{0,1:T(2,128)} %param.12) | copy-start | bytes 388
  31.7 3.7 %copy-start.1 = (bf16[16,896]{1,0:T(8,128)(2,1)S(1)}, bf16[16,896]{1,0:T(8,128)(2,1)}, u32[]{:S(2)}) copy-start(bf16[16,896]{1,0:T(8,128)(2,1)} %param.7) | copy-start | bytes 86020
  31.7 15.7 %copy-start.2 = (bf16[1,896,16]{1,2,0:T(8,128)(2,1)S(1)}, bf16[1,896,16]{1,2,0:T(8,128)(2,1)}, u32[]{:S(2)}) copy-start(bf16[1,896,16]{1,2,0:T(8,128)(2,1)} %param.10) | copy-start | bytes 86020
  36.8 10.7 %all-to-all-start = ((bf16[4,16,896]{2,1,0:T(8,128)(2,1)}), bf16[4,16,896]{2,1,0:T(8,128)(2,1)S(1)}, u32[]{:S(2)}, u32[]{:S(2)}) async-start(bf16[4,16,896]{2,1,0:T(8,128)(2,1)} %bitcast), calls=%async_computation.2 | async-start | bytes 229376 | tf_op jit(solution)/shard_map/all_to_all | solution.py:66
  53.8 22.3 %all-to-all-start.1 = ((bf16[4,16,896]{2,1,0:T(8,128)(2,1)}), bf16[4,16,896]{2,1,0:T(8,128)(2,1)S(1)}, u32[]{:S(2)}, u32[]{:S(2)}) async-start(bf16[4,16,896]{2,1,0:T(8,128)(2,1)} %convolution_convert_fusion.1), calls=%async_computation.3 | async-start | bytes 229376 | tf_op jit(solution)/shard_map/all_to_all | solution.py:74
  57.2 39.0 %reduce-scatter.5.cloned.1.call-start = ((), (), s32[]{:S(2)}) async-start(), calls=%async_computation.5 | async-start | bytes 143360 | tf_op jit(solution)/shard_map/reduce_scatter | solution.py:33
  70.6 5.5 %copy-start.4 = (f32[16,2]{0,1:T(2,128)S(1)}, f32[16,2]{0,1:T(2,128)}, u32[]{:S(2)}) copy-start(f32[16,2]{0,1:T(2,128)} %param.13) | copy-start | bytes 388
Sparse Core Ops, SparseCore 0:
  35.3 27.0 reduce-scatter.2
  76.2 19.9 reduce-scatter.4
